TPU v7x, 256 devices: a whole 4x4x8 slice. The times are simulated.
256 devices in a mesh: expert: 16 (over z, core), shard: 16 (over y, x).
Axes of the slice: x: 4, y: 4, z: 8, core: 2. Of those that a mesh axis runs over, the one named last changes fastest.
Arguments:
- w_down: float32 [64, 1024, 2048], P('expert', None, 'shard'), may hold values from -0.25 to 0.25
- avg_down: float32 [64, 1024, 2048], P('expert', None, 'shard'), may hold values from -0.1875 to 0.1875
- mix_share: float32 [64], P('expert'), may hold values from 0.2 to 0.8
- router_weight: float32 [2048, 64], P('shard', 'expert'), may hold values from -0.125 to 0.125
- router_gain: float32 [2048], P('shard'), may hold values from 0.25 to 1.75
Outputs:
- serve_down: bfloat16 [64, 1024, 2048], P('expert')
- scale_down: float32 [64, 1024], P('expert')
- serve_router: bfloat16 [2048, 64], replicated
All inputs are finite; a program needn't handle non-finite values. Where the computation divides by a largest or mean magnitude, that divisor is 1e-20 or more.
Results may differ from a plain program's by a relative error of at most 0.001.
Values may be sent and summed in bfloat16 or wider, within the bound.
No kernel may reach another device: no remote copies, remote signals or barrier semaphores. Data moves between devices by JAX's collectives and lax.ppermute only.
A program may use at most 128 MiB of HBM per device.

v0:
```python
import jax
import jax.numpy as jnp
from jax import lax
from jax.sharding import PartitionSpec as P

D_MODEL = 2048


def sent_to_all(value, axis):
    copies = jnp.broadcast_to(value, (lax.axis_size(axis), *value.shape))
    return lax.all_to_all(copies, axis, split_axis=0, concat_axis=0, tiled=True)


def taken_together(value, axis):
    everything = sent_to_all(value, axis)
    return jnp.sum(everything, axis=0)


def laid_out(tiles, dim):
    shape = list(tiles.shape[1:])
    shape[dim] *= tiles.shape[0]
    return jnp.moveaxis(tiles, 0, dim).reshape(shape)


def gathered_copies(value, axis, dim):
    return laid_out(sent_to_all(value, axis), dim)


def body(w_down, avg_down, mix_share, router_weight, router_gain):
    fresh_down = mix_share[:, None, None] * w_down + (1.0 - mix_share[:, None, None]) * avg_down
    total_down = taken_together(jnp.sum(jnp.abs(fresh_down), axis=2), "shard")
    scale_down = total_down / D_MODEL
    narrow_down = (fresh_down / jnp.expand_dims(scale_down, 2)).astype(jnp.bfloat16)
    serve_down = lax.all_gather(narrow_down, "shard", axis=2, tiled=True)
    part_router = (router_weight * router_gain[:, None]).astype(jnp.bfloat16)
    row_router = gathered_copies(part_router, "shard", 0)
    serve_router = lax.all_gather(row_router, "expert", axis=1, tiled=True)
    return (serve_down, scale_down, serve_router)


def solution(mesh):
    return jax.shard_map(
        body,
        mesh=mesh,
        in_specs=(
            P("expert", None, "shard"),
            P("expert", None, "shard"),
            P("expert"),
            P("shard", "expert"),
            P("shard"),
        ),
        out_specs=(P("expert", None, None), P("expert", None), P()),
        check_vma=False,
    )
```

profile of v0, /device:TPU:2, one launch (start us, length us, event | category | flops | bytes accessed | tf_op | source)
XLA Modules:
  0.0 174.2 jit_solution(17278753643345742411)
XLA Ops:
  7.2 0.0 all-gather.3.cloned.1.call-start
  7.2 0.7 broadcast_subtract_fusion
  7.9 0.0 copy-start
  7.9 0.0 copy-start.2
  7.9 3.1 %abs_reduce_fusion = f32[4,1024]{1,0:T(4,128)S(1)} fusion(f32[4,1024,128]{2,1,0:T(8,128)} %param.6, f32[4]{0:T(128)S(1)} %broadcast_subtract_fusion, f32[4,1024,128]{2,1,0:T(8,128)} %param.5, f32[4]{0:T(128)} %param.7), kind=kLoop, calls=%fused_computation.1 | loop fusion | flops 2617344 | bytes 4210720 | tf_op jit(solution)/shard_map/reduce_sum | solution.py:31
  11.0 14.6 %all_to_all.10 = f32[16,4,1024]{2,1,0:T(4,128)S(1)} all-to-all(f32[16,4,1024]{2,1,0:T(4,128)S(1)} %broadcast_in_dim.4), channel_id=1, replica_groups=mesh['expert'=16,'shard'=16] {'shard'}, dimensions={0} | all-to-all | bytes 524288 | tf_op jit(solution)/shard_map/all_to_all | solution.py:11
  25.6 0.1 reduce_sum.19
  25.7 0.0 copy-done
  25.7 0.0 copy-done.2
  25.7 0.0 copy-start.1
  25.7 0.0 copy-start.3
  25.7 0.0 copy-start.4
  25.7 2.8 %divide_convert_fusion = bf16[4,1024,128]{2,1,0:T(8,128)(2,1)} fusion(f32[4,1024]{1,0:T(4,128)S(1)} %broadcast_multiply_fusion, f32[4,1024,128]{2,1,0:T(8,128)S(1)} %copy-done, f32[4]{0:T(128)S(1)} %broadcast_subtract_fusion, f32[4,1024,128]{2,1,0:T(8,128)} %param.5, f32[4]{0:T(128)S(1)} %copy-done.2), kind=kLoop, calls=%fused_computation | loop fusion | flops 2621440 | bytes 5259296 | tf_op jit(solution)/shard_map/convert_element_type | solution.py:33
  28.5 0.0 copy-done.1
  28.5 0.0 all-gather.3.cloned.1.call-update
  28.5 0.0 copy-done.3
  28.5 0.0 copy-done.4
  28.6 10.5 %all_to_all.11 = bf16[16,128,4]{1,2,0:T(4,128)(2,1)S(1)} all-to-all(bf16[16,128,4]{1,2,0:T(4,128)(2,1)S(1)} %broadcast_in_dim.5), channel_id=1, replica_groups=mesh['expert'=16,'shard'=16] {'shard'}, dimensions={0} | all-to-all | bytes 32768 | tf_op jit(solution)/shard_map/all_to_all | solution.py:11
  39.1 20.7 %all-gather = bf16[16,4,2048]{2,1,0:T(4,128)(2,1)S(1)} all-gather(bf16[1,4,2048]{2,1,0:T(4,128)(2,1)S(1)} %bitcast.7), channel_id=1, replica_groups=mesh['expert'=16,'shard'=16] {'expert'}, dimensions={0}, use_global_device_ids=true | all-gather | bytes 278528 | tf_op jit(solution)/shard_map/all_gather | solution.py:37
  59.7 0.8 reshape.18
  60.5 92.7 %all-gather.3.cloned.1.call-done = bf16[4,1024,2048]{2,1,0:T(8,128)(2,1)} async-done(((bf16[4,1024,128]{2,1,0:T(8,128)(2,1)}), bf16[4,1024,2048]{2,1,0:T(8,128)(2,1)}) %all-gather.3.cloned.1.call-update) | async-done | bytes 16777232 | tf_op jit(solution)/shard_map/all_gather | solution.py:34
  153.2 14.2 %copy.11 = bf16[4,1024,2048]{2,1,0:T(8,128)(2,1)} copy(bf16[4,1024,2048]{2,1,0:T(8,128)(2,1)} %all-gather.3.cloned.1.call-done) | data formatting | bytes 33554432
  (4 shorter events, 0.1 us)
Async XLA Ops:
  7.2 146.0 %all-gather.3.cloned.1.call-start = ((), (), s32[]{:S(2)}) async-start(), calls=%async_computation.2 | async-start | bytes 17825792 | tf_op jit(solution)/shard_map/all_gather | solution.py:34
  7.9 17.8 %copy-start = (f32[4,1024,128]{2,1,0:T(8,128)S(1)}, f32[4,1024,128]{2,1,0:T(8,128)}, u32[]{:S(2)}) copy-start(f32[4,1024,128]{2,1,0:T(8,128)} %param.6) | copy-start | bytes 6291460
  7.9 17.8 %copy-start.2 = (f32[4]{0:T(128)S(1)}, f32[4]{0:T(128)}, u32[]{:S(2)}) copy-start(f32[4]{0:T(128)} %param.7) | copy-start | bytes 52
  25.7 2.8 %copy-start.1 = (f32[4,1024]{1,0:T(4,128)}, f32[4,1024]{1,0:T(4,128)S(1)}, u32[]{:S(2)}) copy-start(f32[4,1024]{1,0:T(4,128)S(1)} %broadcast_multiply_fusion) | copy-start | bytes 49156
  25.7 2.8 %copy-start.3 = (f32[128,4]{0,1:T(4,128)S(1)}, f32[128,4]{0,1:T(4,128)}, u32[]{:S(2)}) copy-start(f32[128,4]{0,1:T(4,128)} %param.8) | copy-start | bytes 6148
  25.7 2.8 %copy-start.4 = (f32[128]{0:T(128)S(1)}, f32[128]{0:T(128)}, u32[]{:S(2)}) copy-start(f32[128]{0:T(128)} %param.9) | copy-start | bytes 1540
Sparse Core Ops, SparseCore 0:
  28.6 124.4 all-gather.2
where the time goes:
time: 174 us
  waiting for transfers between devices  92.7 us (53%)
  blocking collectives  45.8 us (26%)
  local copies, waits for them, and re-layouts  15 us (9%)
  between operations  14.1 us (8%)
  other arithmetic  6.58 us (4%)
    all_gather x1, waiting for transfers between devices, body(): serve_down = lax.all_gather(narrow_down, 'shard', axis=2, tiled=True)  92.7 us
    all_to_all x2, blocking collectives, sent_to_all(): return lax.all_to_all(copies, axis, split_axis=0, concat_axis=0, tiled=True)  25.1 us
    all_gather x1, blocking collectives, body(): serve_router = lax.all_gather(row_router, 'expert', axis=1, tiled=True)  20.7 us
    unnamed x12, local copies, waits for them, and re-layouts  14.9 us
  transfers between devices with their start and end apart: 1, of which 1 were waited for; matrix products, arithmetic and copies ran while one was open for 0% of the time, Pallas kernels for 0%

commit v1 on v0

--- a/solution.py
+++ b/solution.py
@@ -4,6 +4,12 @@
 from jax.sharding import PartitionSpec as P
 
 D_MODEL = 2048
+
+
+def gather_from_all(x, axis, dim):
+    length = lax.axis_size(axis)
+    repeats = [length if d == dim else 1 for d in range(x.ndim)]
+    return lax.all_to_all(jnp.tile(x, repeats), axis, split_axis=dim, concat_axis=dim, tiled=True)
 
 
 def sent_to_all(value, axis):
@@ -31,7 +37,7 @@
     total_down = taken_together(jnp.sum(jnp.abs(fresh_down), axis=2), "shard")
     scale_down = total_down / D_MODEL
     narrow_down = (fresh_down / jnp.expand_dims(scale_down, 2)).astype(jnp.bfloat16)
-    serve_down = lax.all_gather(narrow_down, "shard", axis=2, tiled=True)
+    serve_down = gather_from_all(narrow_down, "shard", 2)
     part_router = (router_weight * router_gain[:, None]).astype(jnp.bfloat16)
     row_router = gathered_copies(part_router, "shard", 0)
     serve_router = lax.all_gather(row_router, "expert", axis=1, tiled=True)

time: 174 us -> 315 us (1.81); the launches traced: 174 us -> 311 us
  waiting for transfers between devices: 92.7 us -> 228 us
  blocking collectives: 45.8 us -> 20.7 us
  local copies, waits for them, and re-layouts: 15 us -> 36.8 us
  starting transfers between devices: 0.04 us -> 18.5 us
  between operations: 14.1 us -> 0.71 us
    all_to_all x0 -> x3, waiting for transfers between devices: none -> 228 us  [the longest x1 218 us: gather_from_all(): lax.all_to_all(jnp.tile(x, repeats), axis, split_axis=dim, concat_axis=di...]
    all_gather x1 -> x0, waiting for transfers between devices: 92.7 us -> none  [body(): serve_down = lax.all_gather(narrow_down, 'shard', axis=2, tiled=True)]
    all_to_all x2 -> x0, blocking collectives: 25.1 us -> none  [sent_to_all(): return lax.all_to_all(copies, axis, split_axis=0, concat_axis=0, tiled=True)]
    all_to_all x0 -> x3, starting transfers between devices: none -> 18.5 us  [the longest x2 12.2 us: sent_to_all(): return lax.all_to_all(copies, axis, split_axis=0, concat_axis=0, tiled=True)]
    unnamed x12, local copies, waits for them, and re-layouts: 14.9 us -> 26.8 us
    another operation x0 -> x1, local copies, waits for them, and re-layouts: none -> 7.66 us  [gather_from_all(): jnp.tile(x, repeats)]
  transfers between devices with their start and end apart: 1 -> 3, of which waited for: 1 -> 3; matrix products, arithmetic and copies ran while one was open for 0% -> 1% of each run, Pallas kernels for 0% -> 0%
where the time goes in v1:
time: 315 us; the launch traced here: 311 us
  waiting for transfers between devices  228 us (72%)
  local copies, waits for them, and re-layouts  36.8 us (12%)
  blocking collectives  20.7 us (7%)
  starting transfers between devices  18.5 us (6%)
  other arithmetic  5.8 us (2%)
    all_to_all x1, waiting for transfers between devices, gather_from_all(): lax.all_to_all(jnp.tile(x, repeats), axis, split_axis=dim, concat_axis=di...  218 us
    unnamed x12, local copies, waits for them, and re-layouts  26.8 us
    all_gather x1, blocking collectives, body(): serve_router = lax.all_gather(row_router, 'expert', axis=1, tiled=True)  20.7 us
    all_to_all x2, starting transfers between devices, sent_to_all(): return lax.all_to_all(copies, axis, split_axis=0, concat_axis=0, tiled=True)  12.2 us
    all_to_all x2, waiting for transfers between devices, sent_to_all(): return lax.all_to_all(copies, axis, split_axis=0, concat_axis=0, tiled=True)  10.6 us
    another operation x1, local copies, waits for them, and re-layouts, gather_from_all(): jnp.tile(x, repeats)  7.66 us
    all_to_all x1, starting transfers between devices, gather_from_all(): lax.all_to_all(jnp.tile(x, repeats), axis, split_axis=dim, concat_axis=di...  6.32 us
  transfers between devices with their start and end apart: 3, of which 3 were waited for; matrix products, arithmetic and copies ran while one was open for 1% of the time, Pallas kernels for 0%

profile of v1, /device:TPU:2, one launch (start us, length us, event | category | flops | bytes accessed | tf_op | source)
XLA Modules:
  0.0 310.9 jit_solution(11970901923644132086)
XLA Ops:
  0.6 0.7 broadcast_subtract_fusion
  1.3 0.0 copy-start.3
  1.3 3.1 abs_reduce_fusion
  4.4 0.8 broadcast_in_dim.4
  5.1 7.5 %all-to-all-start = ((f32[16,4,1024]{2,1,0:T(4,128)}), f32[16,4,1024]{2,1,0:T(4,128)S(1)}, u32[]{:S(2)}, u32[]{:S(2)}) async-start(f32[16,4,1024]{2,1,0:T(4,128)} %broadcast_in_dim.4), calls=%async_computation | async-start | bytes 524288 | tf_op jit(solution)/shard_map/all_to_all | solution.py:17
  12.6 0.0 copy-done.3
  12.6 0.0 copy-done.4
  12.6 7.3 %all-to-all-done = f32[16,4,1024]{2,1,0:T(4,128)S(1)} async-done(((f32[16,4,1024]{2,1,0:T(4,128)}), f32[16,4,1024]{2,1,0:T(4,128)S(1)}, u32[]{:S(2)}, u32[]{:S(2)}) %all-to-all-start) | async-done | bytes 262176 | tf_op jit(solution)/shard_map/all_to_all | solution.py:17
  20.0 0.6 broadcast_in_dim.5
  20.6 4.7 %all-to-all-start.2 = ((bf16[16,128,4]{1,2,0:T(4,128)(2,1)}), bf16[16,128,4]{1,2,0:T(4,128)(2,1)S(1)}, u32[]{:S(2)}, u32[]{:S(2)}) async-start(bf16[16,128,4]{1,2,0:T(4,128)(2,1)} %broadcast_in_dim.5), calls=%async_computation.2 | async-start | bytes 32768 | tf_op jit(solution)/shard_map/all_to_all | solution.py:17
  25.3 0.1 reduce_sum.19
  25.4 0.0 copy-done
  25.4 0.0 copy-done.2
  25.4 0.0 copy-start.1
  25.4 2.0 divide_convert_fusion
  27.4 0.0 copy-done.1
  27.4 0.9 copy.13
  28.3 3.3 %all-to-all-done.2 = bf16[16,128,4]{1,2,0:T(4,128)(2,1)S(1)} async-done(((bf16[16,128,4]{1,2,0:T(4,128)(2,1)}), bf16[16,128,4]{1,2,0:T(4,128)(2,1)S(1)}, u32[]{:S(2)}, u32[]{:S(2)}) %all-to-all-start.2) | async-done | bytes 16416 | tf_op jit(solution)/shard_map/all_to_all | solution.py:17
  31.6 7.7 %tile.4 = bf16[4,1024,16,128]{1,0,3,2:T(4,128)(2,1)} broadcast(bf16[4,1024,128]{1,0,2:T(4,128)(2,1)S(1)} %copy.13), dimensions={0,1,3} | broadcast | bytes 17825792 | tf_op jit(solution)/shard_map/tile | solution.py:12
  39.3 6.3 %all-to-all-start.1 = ((bf16[4,1024,2048]{1,0,2:T(4,128)(2,1)}), bf16[4,1024,2048]{1,0,2:T(4,128)(2,1)}, u32[]{:S(2)}, u32[]{:S(2)}) async-start(bf16[4,1024,2048]{1,0,2:T(4,128)(2,1)} %bitcast.7), calls=%async_computation.1 | async-start | bytes 33554432 | tf_op jit(solution)/shard_map/all_to_all | solution.py:12
  45.6 20.7 %all-gather = bf16[16,4,2048]{2,1,0:T(4,128)(2,1)S(1)} all-gather(bf16[1,4,2048]{2,1,0:T(4,128)(2,1)S(1)} %bitcast.9), channel_id=1, replica_groups=mesh['expert'=16,'shard'=16] {'expert'}, dimensions={0}, use_global_device_ids=true | all-gather | bytes 278528 | tf_op jit(solution)/shard_map/all_gather | solution.py:43
  66.2 0.8 reshape.22
  67.0 217.9 %all-to-all-done.1 = bf16[4,1024,2048]{1,0,2:T(4,128)(2,1)} async-done(((bf16[4,1024,2048]{1,0,2:T(4,128)(2,1)}), bf16[4,1024,2048]{1,0,2:T(4,128)(2,1)}, u32[]{:S(2)}, u32[]{:S(2)}) %all-to-all-start.1) | async-done | bytes 16777248 | tf_op jit(solution)/shard_map/all_to_all | solution.py:12
  284.9 26.0 %copy.14 = bf16[4,1024,2048]{2,1,0:T(8,128)(2,1)} copy(bf16[4,1024,2048]{1,0,2:T(4,128)(2,1)} %all-to-all-done.1) | data formatting | bytes 33554432
  (5 shorter events, 0.0 us)
Async XLA Ops:
  1.3 11.3 %copy-start.3 = (f32[128,4]{0,1:T(4,128)S(1)}, f32[128,4]{0,1:T(4,128)}, u32[]{:S(2)}) copy-start(f32[128,4]{0,1:T(4,128)} %param.8) | copy-start | bytes 6148
  1.3 11.3 %copy-start.4 = (f32[128]{0:T(128)S(1)}, f32[128]{0:T(128)}, u32[]{:S(2)}) copy-start(f32[128]{0:T(128)} %param.9) | copy-start | bytes 1540
  1.3 24.1 %copy-start = (f32[4,1024,128]{2,1,0:T(8,128)S(1)}, f32[4,1024,128]{2,1,0:T(8,128)}, u32[]{:S(2)}) copy-start(f32[4,1024,128]{2,1,0:T(8,128)} %param.6) | copy-start | bytes 6291460
  1.3 24.1 %copy-start.2 = (f32[4]{0:T(128)S(1)}, f32[4]{0:T(128)}, u32[]{:S(2)}) copy-start(f32[4]{0:T(128)} %param.7) | copy-start | bytes 52
  5.1 14.8 %all-to-all-start = ((f32[16,4,1024]{2,1,0:T(4,128)}), f32[16,4,1024]{2,1,0:T(4,128)S(1)}, u32[]{:S(2)}, u32[]{:S(2)}) async-start(f32[16,4,1024]{2,1,0:T(4,128)} %broadcast_in_dim.4), calls=%async_computation | async-start | bytes 524288 | tf_op jit(solution)/shard_map/all_to_all | solution.py:17
  20.6 11.0 %all-to-all-start.2 = ((bf16[16,128,4]{1,2,0:T(4,128)(2,1)}), bf16[16,128,4]{1,2,0:T(4,128)(2,1)S(1)}, u32[]{:S(2)}, u32[]{:S(2)}) async-start(bf16[16,128,4]{1,2,0:T(4,128)(2,1)} %broadcast_in_dim.5), calls=%async_computation.2 | async-start | bytes 32768 | tf_op jit(solution)/shard_map/all_to_all | solution.py:17
  25.4 2.0 copy-start.1
  39.3 245.6 %all-to-all-start.1 = ((bf16[4,1024,2048]{1,0,2:T(4,128)(2,1)}), bf16[4,1024,2048]{1,0,2:T(4,128)(2,1)}, u32[]{:S(2)}, u32[]{:S(2)}) async-start(bf16[4,1024,2048]{1,0,2:T(4,128)(2,1)} %bitcast.7), calls=%async_computation.1 | async-start | bytes 33554432 | tf_op jit(solution)/shard_map/all_to_all | solution.py:12
